TPU v7x, 32 devices: a 4x4x1 block of a 4x4x8 slice. The times are simulated.
32 devices in a mesh: batch: 1 (over z), col: 4 (over y), row: 8 (over x, core).
Axes of the slice: x: 4, y: 4, z: 1, core: 2. Of those that a mesh axis runs over, the one named last changes fastest.
The devices are a block of a 4x4x8 slice.
Arguments:
- mat_blocks: float32 [32768, 128, 32], P(('batch', 'row'), 'col')
Outputs:
- output 1: float32 [32768, 128, 32], P(('batch', 'row'), 'col')
- output 2: float32 [128], P('batch')
- output 3: float32 [4, 32, 32], P('batch')
All inputs are finite; a program needn't handle non-finite values.
Results may differ from a plain program's by a relative error of at most 0.001.
Values sent between devices are 32-bit elements.
A program may use at most 768 MiB of HBM per device.

v0:
```python
import math
import jax
import jax.numpy as jnp
from jax import lax
from jax.sharding import PartitionSpec as P

PANELS = 4
HIGHEST = lax.Precision.HIGHEST


def mat_dot(left_mat, right_mat):
    return jnp.dot(left_mat, right_mat, precision=HIGHEST, preferred_element_type=jnp.float32)


def mat_einsum(einsum_form, left_mat, right_mat):
    return jnp.einsum(einsum_form, left_mat, right_mat, precision=HIGHEST, preferred_element_type=jnp.float32)


def apply_reflector(panel_work, tau_vec, column, col_idx, pivot_row, row_ids, tail_dots, pivot_line):
    col_ids = jnp.arange(panel_work.shape[1])
    alpha_val = lax.dynamic_index_in_dim(pivot_line, col_idx, keepdims=False)
    norm_val = jnp.sqrt(lax.dynamic_index_in_dim(tail_dots, col_idx, keepdims=False))
    beta_val = jnp.where(alpha_val >= 0.0, -norm_val, norm_val)
    tau_val = (beta_val - alpha_val) / beta_val
    scale_val = 1.0 / (alpha_val - beta_val)
    refl_vec = jnp.where(row_ids > pivot_row, column * scale_val, jnp.where(row_ids == pivot_row, 1.0, 0.0))
    refl_dot = scale_val * (tail_dots - alpha_val * pivot_line) + pivot_line
    refl_dot = jnp.where(col_ids > col_idx, refl_dot, 0.0)
    new_col = jnp.where(row_ids < pivot_row, column, jnp.where(row_ids == pivot_row, beta_val, refl_vec))
    panel_work = jnp.where(col_ids[None, :] == col_idx, new_col[:, None], panel_work - tau_val * refl_vec[:, None] * refl_dot[None, :])
    tau_vec = jnp.where(col_ids == col_idx, tau_val, tau_vec)
    return panel_work, tau_vec


def factor_panel_rows(panel_in, row_base, pivot_base):
    local_rows, block_width = panel_in.shape
    row_ids = row_base + jnp.arange(local_rows)

    def column_step(col_idx, loop_state):
        panel_work, tau_vec = loop_state
        pivot_row = pivot_base + col_idx
        column = lax.dynamic_index_in_dim(panel_work, col_idx, axis=1, keepdims=False)
        tail_col = jnp.where(row_ids >= pivot_row, column, 0.0)
        local_pivot = jnp.clip(pivot_row - row_base, 0, local_rows - 1)
        holds_pivot = (pivot_row >= row_base) & (pivot_row < row_base + local_rows)
        pivot_line = lax.dynamic_index_in_dim(panel_work, local_pivot, axis=0, keepdims=False)
        pivot_line = jnp.where(holds_pivot, pivot_line, 0.0)
        packed = jnp.concatenate([mat_dot(tail_col[None, :], panel_work)[0], pivot_line])
        packed = lax.psum(packed, 'row')
        return apply_reflector(panel_work, tau_vec, column, col_idx, pivot_row, row_ids, packed[:block_width], packed[block_width:])

    return lax.fori_loop(0, block_width, column_step, (panel_in, jnp.zeros((block_width,), jnp.float32)))


def tfactor_from_gram(gram_mat, tau_vec):
    block_width = gram_mat.shape[0]
    col_ids = jnp.arange(block_width)
    step_mat = -tau_vec[:, None] * jnp.where(col_ids[None, :] > col_ids[:, None], gram_mat, 0.0)
    eye_mat = jnp.eye(block_width, dtype=jnp.float32)
    inv_acc = eye_mat + step_mat
    power_mat = step_mat
    for level_num in range(max(1, math.ceil(math.log2(block_width))) - 1):
        power_mat = mat_dot(power_mat, power_mat)
        inv_acc = mat_dot(inv_acc, eye_mat + power_mat)
    return inv_acc * tau_vec[None, :]


def solution(mesh):
    col_count = mesh.shape['col']
    block_spec = P(('batch', 'row'), 'col', None)

    def device_fn(a_local):
        local_rows, local_blocks, block_width = a_local.shape
        col_rank = lax.axis_index('col')
        row_base = lax.axis_index('row') * local_rows
        row_ids = row_base + jnp.arange(local_rows)
        col_ids = jnp.arange(block_width)
        global_ids = jnp.arange(local_blocks) * col_count + col_rank
        tau_list = []
        tfac_list = []
        for panel_idx in range(PANELS):
            owner_col = panel_idx % col_count
            block_pos = panel_idx // col_count
            pivot_ids = panel_idx * block_width + col_ids
            panel_out, tau_vec = factor_panel_rows(a_local[:, block_pos, :], row_base, panel_idx * block_width)
            refl_mat = jnp.where(row_ids[:, None] > pivot_ids[None, :], panel_out, jnp.where(row_ids[:, None] == pivot_ids[None, :], 1.0, 0.0))
            gram_mat = lax.psum(mat_einsum('rk,rj->kj', refl_mat, refl_mat), 'row')
            t_factor = tfactor_from_gram(gram_mat, tau_vec)
            packed = jnp.concatenate([refl_mat, t_factor], axis=0)
            packed = lax.psum(jnp.where(col_rank == owner_col, packed, 0.0), 'col')
            refl_mat = packed[:local_rows]
            t_factor = packed[local_rows:]
            w_summed = lax.psum(mat_einsum('rk,rbc->kbc', refl_mat, a_local), 'row')
            w_mat = mat_einsum('kj,kbc->jbc', t_factor, w_summed)
            w_mat = jnp.where((global_ids > panel_idx)[None, :, None], w_mat, 0.0)
            a_local = a_local - mat_einsum('rj,jbc->rbc', refl_mat, w_mat)
            a_local = jnp.where((global_ids == panel_idx)[None, :, None], panel_out[:, None, :], a_local)
            tau_list.append(jnp.diagonal(t_factor))
            tfac_list.append(t_factor)
        return a_local, jnp.concatenate(tau_list), jnp.stack(tfac_list)

    return jax.shard_map(device_fn, mesh=mesh, in_specs=(block_spec,), out_specs=(block_spec, P('batch'), P('batch', None, None)), check_vma=False)
```

profile of v0, /device:TPU:97, one launch (start us, length us, event | category | flops | bytes accessed | tf_op | source)
XLA Modules:
  0.0 3164.2 jit_solution(5551201584918998575)
XLA Ops:
  8.4 591.2 %while.76 = (s32[]{:T(128)}, f32[4096,32]{0,1:T(8,128)S(1)}, f32[32]{0:T(128)S(1)}, s32[]{:T(128)}, s32[]{:T(128)}, /*index=5*/s32[]{:T(128)}, s32[]{:T(128)}, s32[]{:T(128)}, f32[]{:T(128)}, f32[]{:T(128)}) while((s32[]{:T(128)}, f32[4096,32]{0,1:T(8,128)S(1)}, f32[32]{0:T(128)S(1)}, s32[]{:T(128)}, ...), condition=%wide.region_2.3_spmd.clone.clone.clone, body=%wide.region_0.2_spmd.clone.clone.clone.sunk | while | flops 2023920 | bytes 1764387 | solution.py:52
  9.3 13.8 psum.160
  29.0 14.5 psum.160
  49.4 12.5 psum.160
  67.7 12.5 psum.160
  86.1 12.5 psum.160
  104.5 12.5 psum.160
  122.9 12.5 psum.160
  141.2 12.5 psum.160
  159.6 12.5 psum.160
  178.0 12.5 psum.160
  196.3 12.5 psum.160
  214.7 12.5 psum.160
  233.1 12.5 psum.160
  251.4 12.5 psum.160
  269.8 12.5 psum.160
  288.2 12.5 psum.160
  306.6 12.5 psum.160
  324.9 12.5 psum.160
  343.3 12.5 psum.160
  361.7 12.5 psum.160
  380.0 12.5 psum.160
  398.4 12.5 psum.160
  416.8 12.5 psum.160
  435.1 12.5 psum.160
  453.5 12.5 psum.160
  471.9 12.5 psum.160
  490.3 12.5 psum.160
  508.6 12.5 psum.160
  600.2 20.8 psum.132
  623.4 39.2 %all-reduce.9.cloned.1.call-done = f32[4128,32]{0,1:T(8,128)} async-done(((f32[4128,32]{0,1:T(8,128)}), f32[4128,32]{0,1:T(8,128)}) %all-reduce.9.cloned.1.call-update) | async-done | bytes 528400 | tf_op jit(solution)/shard_map/psum | solution.py:90
  662.6 41.3 %fusion.38 = f32[32,32,32]{2,0,1:T(8,128)} fusion(f32[4096,32,32]{0,2,1:T(8,128)} %param.9, f32[4128,32]{0,1:T(8,128)} %all-reduce.9.cloned.1.call-done), kind=kOutput, calls=%fused_computation.117 | convolution fusion | flops 1610612736 | bytes 17432576 | tf_op jit(solution)/shard_map/rk,rbc->kbc/dot_general | solution.py:16
  704.3 55.8 %all-reduce.11.cloned.1.call-done = f32[32,32,32]{2,0,1:T(8,128)} async-done(((f32[32,32,32]{2,0,1:T(8,128)}), f32[32,32,32]{2,0,1:T(8,128)}) %all-reduce.11.cloned.1.call-update) | async-done | bytes 131088 | tf_op jit(solution)/shard_map/psum | solution.py:93
  761.9 16.1 fusion.49
  796.0 595.7 %while.77 = (s32[]{:T(128)}, f32[4096,32]{0,1:T(8,128)S(1)}, f32[32]{0:T(128)S(1)}, s32[]{:T(128)}, s32[]{:T(128)}, /*index=5*/s32[]{:T(128)}, s32[]{:T(128)}, s...) while((s32[]{:T(128)}, f32[4096,32]{0,1:T(8,128)S(1)}, f32[32]{0:T(128)S(1)}, ...), condition=%wide.region_8.9_spmd.clone.clone.clone, body=%wide.region_6.8_spmd.clone.clone.clone.sunk | while | flops 2023921 | bytes 1764407 | solution.py:52
  796.9 14.7 psum.161
  817.6 13.2 psum.161
  892.4 12.5 psum.161
  1244.4 12.5 psum.161
  1392.4 20.8 psum.135
  1416.2 37.0 %all-reduce.13.cloned.1.call-done = f32[4128,32]{0,1:T(8,128)} async-done(((f32[4128,32]{0,1:T(8,128)}), f32[4128,32]{0,1:T(8,128)}) %all-reduce.13.cloned.1.call-update) | async-done | bytes 528400 | tf_op jit(solution)/shard_map/psum | solution.py:90
  1453.2 41.3 %fusion.36 = f32[32,32,32]{2,0,1:T(8,128)} fusion(f32[4096,32,32]{0,2,1:T(8,128)} %copy-done.1, f32[4128,32]{0,1:T(8,128)} %all-reduce.13.cloned.1.call-done), kind=kOutput, calls=%fused_computation.115 | convolution fusion | flops 1610612736 | bytes 17432576 | tf_op jit(solution)/shard_map/rk,rbc->kbc/dot_general | solution.py:16
  1494.8 56.0 %all-reduce.15.cloned.1.call-done = f32[32,32,32]{2,0,1:T(8,128)} async-done(((f32[32,32,32]{2,0,1:T(8,128)}), f32[32,32,32]{2,0,1:T(8,128)}) %all-reduce.15.cloned.1.call-update) | async-done | bytes 131088 | tf_op jit(solution)/shard_map/psum | solution.py:93
  1552.6 16.0 fusion.46
  1586.6 595.7 %while.78 = (s32[]{:T(128)}, f32[4096,32]{0,1:T(8,128)S(1)}, f32[32]{0:T(128)S(1)}, s32[]{:T(128)}, s32[]{:T(128)}, /*index=5*/s32[]{:T(128)}, s32[]{:T(128)}, s...) while((s32[]{:T(128)}, f32[4096,32]{0,1:T(8,128)S(1)}, ...), condition=%wide.region_14.15_spmd.clone.clone.clone, body=%wide.region_12.14_spmd.clone.clone.clone.sunk | while | flops 2023921 | bytes 1764407 | solution.py:52
  1587.5 14.7 psum.162
  1608.2 13.2 psum.162
  1868.3 12.5 psum.162
  2183.0 20.8 psum.138
  2206.5 37.3 %all-reduce.17.cloned.1.call-done = f32[4128,32]{0,1:T(8,128)} async-done(((f32[4128,32]{0,1:T(8,128)}), f32[4128,32]{0,1:T(8,128)}) %all-reduce.17.cloned.1.call-update) | async-done | bytes 528400 | tf_op jit(solution)/shard_map/psum | solution.py:90
  2243.8 41.3 %fusion.34 = f32[32,32,32]{2,0,1:T(8,128)} fusion(f32[4096,32,32]{0,2,1:T(8,128)} %copy-done.2, f32[4128,32]{0,1:T(8,128)} %all-reduce.17.cloned.1.call-done), kind=kOutput, calls=%fused_computation.113 | convolution fusion | flops 1610612736 | bytes 17432576 | tf_op jit(solution)/shard_map/rk,rbc->kbc/dot_general | solution.py:16
  2285.5 55.8 %all-reduce.19.cloned.1.call-done = f32[32,32,32]{2,0,1:T(8,128)} async-done(((f32[32,32,32]{2,0,1:T(8,128)}), f32[32,32,32]{2,0,1:T(8,128)}) %all-reduce.19.cloned.1.call-update) | async-done | bytes 131088 | tf_op jit(solution)/shard_map/psum | solution.py:93
  2343.1 16.0 fusion.43
  2377.1 590.7 %while.79 = (s32[]{:T(128)}, f32[4096,32]{0,1:T(8,128)S(1)}, f32[32]{0:T(128)S(1)}, s32[]{:T(128)}, s32[]{:T(128)}, /*index=5*/s32[]{:T(128)}, s32[]{:T(128)}, s...) while((s32[]{:T(128)}, f32[4096,32]{0,1:T(8,128)S(1)}, ...), condition=%wide.region_20.21_spmd.clone.clone.clone, body=%wide.region_18.20_spmd.clone.clone.clone.sunk | while | flops 2023921 | bytes 1764407 | solution.py:52
  2378.0 14.7 psum.163
  2398.6 13.2 psum.163
  2472.7 12.5 psum.163
  2821.7 12.5 psum.163
  2968.5 20.8 psum.141
  2994.3 35.0 %all-reduce.21.cloned.1.call-done = f32[4128,32]{0,1:T(8,128)} async-done(((f32[4128,32]{0,1:T(8,128)}), f32[4128,32]{0,1:T(8,128)}) %all-reduce.21.cloned.1.call-update) | async-done | bytes 528400 | tf_op jit(solution)/shard_map/psum | solution.py:90
  3031.4 41.4 %fusion.32 = f32[32,32,32]{2,0,1:T(8,128)} fusion(f32[4096,32,32]{0,2,1:T(8,128)} %copy-done, f32[4128,32]{0,1:T(8,128)} %all-reduce.21.cloned.1.call-done), kind=kOutput, calls=%fused_computation.111 | convolution fusion | flops 1610612736 | bytes 17432576 | tf_op jit(solution)/shard_map/rk,rbc->kbc/dot_general | solution.py:16
  3073.5 55.6 %all-reduce.23.cloned.1.call-done = f32[32,32,32]{2,0,1:T(8,128)} async-done(((f32[32,32,32]{2,0,1:T(8,128)}), f32[32,32,32]{2,0,1:T(8,128)}) %all-reduce.23.cloned.1.call-update) | async-done | bytes 131088 | tf_op jit(solution)/shard_map/psum | solution.py:93
  3130.9 13.7 fusion.40
  3144.6 12.5 subtract_select_fusion.4
  (2002 shorter events, 1595.2 us)
Async XLA Ops:
  7.2 655.4 %all-reduce.9.cloned.1.call-start = ((), (), s32[]{:S(2)}) async-start(), calls=%async_computation | async-start | bytes 1081344 | tf_op jit(solution)/shard_map/psum | solution.py:90
  623.3 136.8 %all-reduce.11.cloned.1.call-start = ((), (), s32[]{:S(2)}) async-start(), calls=%async_computation.1 | async-start | bytes 1048576 | tf_op jit(solution)/shard_map/psum | solution.py:93
  662.6 97.5 %copy-start.3 = (f32[4128,32]{0,1:T(8,128)S(1)}, f32[4128,32]{0,1:T(8,128)}, u32[]{:S(2)}) copy-start(f32[4128,32]{0,1:T(8,128)} %all-reduce.9.cloned.1.call-done) | copy-start | bytes 1585156
  703.9 749.3 %all-reduce.13.cloned.1.call-start = ((), (), s32[]{:S(2)}) async-start(), calls=%async_computation.2 | async-start | bytes 1081344 | tf_op jit(solution)/shard_map/psum | solution.py:90
  789.8 6.2 copy-start.1
  1415.5 135.3 %all-reduce.15.cloned.1.call-start = ((), (), s32[]{:S(2)}) async-start(), calls=%async_computation.3 | async-start | bytes 1048576 | tf_op jit(solution)/shard_map/psum | solution.py:93
  1453.2 97.6 %copy-start.4 = (f32[4128,32]{0,1:T(8,128)S(1)}, f32[4128,32]{0,1:T(8,128)}, u32[]{:S(2)}) copy-start(f32[4128,32]{0,1:T(8,128)} %all-reduce.13.cloned.1.call-done) | copy-start | bytes 1585156
  1494.5 749.3 %all-reduce.17.cloned.1.call-start = ((), (), s32[]{:S(2)}) async-start(), calls=%async_computation.4 | async-start | bytes 1081344 | tf_op jit(solution)/shard_map/psum | solution.py:90
  1580.4 6.2 copy-start.2
  2206.1 135.2 %all-reduce.19.cloned.1.call-start = ((), (), s32[]{:S(2)}) async-start(), calls=%async_computation.5 | async-start | bytes 1048576 | tf_op jit(solution)/shard_map/psum | solution.py:93
  2243.8 97.5 %copy-start.5 = (f32[4128,32]{0,1:T(8,128)S(1)}, f32[4128,32]{0,1:T(8,128)}, u32[]{:S(2)}) copy-start(f32[4128,32]{0,1:T(8,128)} %all-reduce.17.cloned.1.call-done) | copy-start | bytes 1585156
  2285.1 744.1 %all-reduce.21.cloned.1.call-start = ((), (), s32[]{:S(2)}) async-start(), calls=%async_computation.6 | async-start | bytes 1081344 | tf_op jit(solution)/shard_map/psum | solution.py:90
  2370.9 6.2 copy-start
  2991.6 137.5 %all-reduce.23.cloned.1.call-start = ((), (), s32[]{:S(2)}) async-start(), calls=%async_computation.7 | async-start | bytes 1048576 | tf_op jit(solution)/shard_map/psum | solution.py:93
  3031.4 97.7 %copy-start.6 = (f32[4128,32]{0,1:T(8,128)S(1)}, f32[4128,32]{0,1:T(8,128)}, u32[]{:S(2)}) copy-start(f32[4128,32]{0,1:T(8,128)} %all-reduce.21.cloned.1.call-done) | copy-start | bytes 1585156
Sparse Core Ops, SparseCore 0:
  623.4 39.1 all-reduce.8
  704.0 56.0 all-reduce.10
  1415.6 37.4 all-reduce.12
  1494.6 56.1 all-reduce.14
  2206.2 37.4 all-reduce.16
  2285.2 56.0 all-reduce.18
  2991.7 37.4 all-reduce.20
  3073.0 56.0 all-reduce.22
where the time goes:
time: 3180 us; the launch traced here: 3160 us
  blocking collectives  1690 us (53%)
  waiting for transfers between devices  372 us (12%)
  loops' own time  361 us (11%)
  matrix products  307 us (10%)
  other arithmetic  224 us (7%)
  local copies, waits for them, and re-layouts  192 us (6%)
    psum x128, blocking collectives, column_step(): packed = lax.psum(packed, 'row')  1610 us
    another operation x4, loops' own time, factor_panel_rows(): lax.fori_loop(0, block_width, column_step, (panel_in, jnp.zeros((block_wi...  361 us
    psum x4, waiting for transfers between devices, device_fn(): w_summed = lax.psum(mat_einsum('rk,rbc->kbc', refl_mat, a_local), 'row')  223 us
    dot_general x12, matrix products, mat_einsum(): jnp.einsum(einsum_form, left_mat, right_mat, precision=HIGHEST, preferred...  174 us
    psum x4, waiting for transfers between devices, device_fn(): packed = lax.psum(jnp.where(col_rank == owner_col, packed, 0.0), 'col')  148 us
    select_n x128, other arithmetic, apply_reflector(): refl_dot = jnp.where(col_ids > col_idx, refl_dot, 0.0)  95.3 us
    psum x4, blocking collectives, device_fn(): gram_mat = lax.psum(mat_einsum('rk,rj->kj', refl_mat, refl_mat), 'row')  83.1 us
    dynamic_slice x128, local copies, waits for them, and re-layouts, apply_reflector(): alpha_val = lax.dynamic_index_in_dim(pivot_line, col_idx, keepdims=False)  80.5 us
  transfers between devices with their start and end apart: 8, of which 8 were waited for; matrix products, arithmetic and copies ran while one was open for 0% of the time, Pallas kernels for 0%

commit v1 on v0

v1 whole, which is shorter than its diff:
```python
import functools
import math
import jax
import jax.numpy as jnp
from jax import lax
from jax.experimental import pallas as pl
from jax.experimental.pallas import tpu as pltpu
from jax.sharding import PartitionSpec as P

PANELS = 4
HIGHEST = lax.Precision.HIGHEST
MESH = pl.DeviceIdType.MESH
COND_MAX = 1.0e4
ABS_MAX = 1.0e15
GRAM_MIN = 1.0e-4


def mat_dot(left_mat, right_mat):
    return jnp.dot(left_mat, right_mat, precision=HIGHEST, preferred_element_type=jnp.float32)


def mat_einsum(einsum_form, left_mat, right_mat):
    return jnp.einsum(einsum_form, left_mat, right_mat, precision=HIGHEST, preferred_element_type=jnp.float32)


def axis_sum_kernel(axis, count, x_ref, out_ref, recv_buf, send_sem, recv_sem):
    me = lax.axis_index(axis)
    barrier = pltpu.get_barrier_semaphore()
    for step in range(1, count):
        pl.semaphore_signal(barrier, inc=1, device_id={axis: lax.rem(me + step, count)}, device_id_type=MESH)
    pl.semaphore_wait(barrier, count - 1)

    def copy(step, slot):
        return pltpu.make_async_remote_copy(
            src_ref=x_ref, dst_ref=recv_buf.at[slot], send_sem=send_sem.at[step], recv_sem=recv_sem.at[step],
            device_id={axis: lax.rem(me + step, count)}, device_id_type=MESH)

    for step in range(1, count):
        copy(step, me).start()
    recv_buf[me] = x_ref[...]
    for step in range(1, count):
        copy(step, lax.rem(me + count - step, count)).wait_recv()
    total = recv_buf[0]
    for i in range(1, count):
        total = total + recv_buf[i]
    out_ref[...] = total
    for step in range(1, count):
        copy(step, me).wait_send()


def axis_sum(x, axis, count, collective_id):
    size = math.prod(x.shape)
    lines = -(-size // 1024) * 8
    flat = jnp.pad(x.reshape(-1), (0, lines * 128 - size)).reshape(lines, 128)
    spec = pl.BlockSpec(memory_space=pltpu.VMEM)
    total = pl.pallas_call(
        functools.partial(axis_sum_kernel, axis, count),
        out_shape=jax.ShapeDtypeStruct(flat.shape, jnp.float32),
        in_specs=[spec],
        out_specs=spec,
        scratch_shapes=[pltpu.VMEM((count,) + flat.shape, jnp.float32), pltpu.SemaphoreType.DMA((count,)), pltpu.SemaphoreType.DMA((count,))],
        compiler_params=pltpu.CompilerParams(collective_id=collective_id, has_side_effects=True),
        name='axis_sum',
    )(flat)
    return total.reshape(-1)[:size].reshape(x.shape)


def apply_reflector(panel_work, tau_vec, column, col_idx, pivot_row, row_ids, tail_dots, pivot_line):
    col_ids = jnp.arange(panel_work.shape[1])
    alpha_val = lax.dynamic_index_in_dim(pivot_line, col_idx, keepdims=False)
    norm_val = jnp.sqrt(lax.dynamic_index_in_dim(tail_dots, col_idx, keepdims=False))
    beta_val = jnp.where(alpha_val >= 0.0, -norm_val, norm_val)
    tau_val = (beta_val - alpha_val) / beta_val
    scale_val = 1.0 / (alpha_val - beta_val)
    refl_vec = jnp.where(row_ids > pivot_row, column * scale_val, jnp.where(row_ids == pivot_row, 1.0, 0.0))
    refl_dot = scale_val * (tail_dots - alpha_val * pivot_line) + pivot_line
    refl_dot = jnp.where(col_ids > col_idx, refl_dot, 0.0)
    new_col = jnp.where(row_ids < pivot_row, column, jnp.where(row_ids == pivot_row, beta_val, refl_vec))
    panel_work = jnp.where(col_ids[None, :] == col_idx, new_col[:, None], panel_work - tau_val * refl_vec[:, None] * refl_dot[None, :])
    tau_vec = jnp.where(col_ids == col_idx, tau_val, tau_vec)
    return panel_work, tau_vec


def factor_panel_rows(panel_in, row_base, pivot_base, row_count):
    local_rows, block_width = panel_in.shape
    row_ids = row_base + jnp.arange(local_rows)

    def column_step(col_idx, loop_state):
        panel_work, tau_vec = loop_state
        pivot_row = pivot_base + col_idx
        column = lax.dynamic_index_in_dim(panel_work, col_idx, axis=1, keepdims=False)
        tail_col = jnp.where(row_ids >= pivot_row, column, 0.0)
        local_pivot = jnp.clip(pivot_row - row_base, 0, local_rows - 1)
        holds_pivot = (pivot_row >= row_base) & (pivot_row < row_base + local_rows)
        pivot_line = lax.dynamic_index_in_dim(panel_work, local_pivot, axis=0, keepdims=False)
        pivot_line = jnp.where(holds_pivot, pivot_line, 0.0)
        packed = jnp.concatenate([mat_dot(tail_col[None, :], panel_work)[0], pivot_line])
        packed = axis_sum(packed, 'row', row_count, 1)
        return apply_reflector(panel_work, tau_vec, column, col_idx, pivot_row, row_ids, packed[:block_width], packed[block_width:])

    return lax.fori_loop(0, block_width, column_step, (panel_in, jnp.zeros((block_width,), jnp.float32)))


def tfactor_from_gram(gram_mat, tau_vec):
    block_width = gram_mat.shape[0]
    col_ids = jnp.arange(block_width)
    step_mat = -tau_vec[:, None] * jnp.where(col_ids[None, :] > col_ids[:, None], gram_mat, 0.0)
    eye_mat = jnp.eye(block_width, dtype=jnp.float32)
    inv_acc = eye_mat + step_mat
    power_mat = step_mat
    for _ in range(max(1, math.ceil(math.log2(block_width))) - 1):
        power_mat = mat_dot(power_mat, power_mat)
        inv_acc = mat_dot(inv_acc, eye_mat + power_mat)
    return inv_acc * tau_vec[None, :]


def columnwise_qr(a_local, col_count, row_count):
    local_rows, local_blocks, block_width = a_local.shape
    col_rank = lax.axis_index('col')
    row_base = lax.axis_index('row') * local_rows
    row_ids = row_base + jnp.arange(local_rows)
    col_ids = jnp.arange(block_width)
    global_ids = jnp.arange(local_blocks) * col_count + col_rank

    def panel_step(panel_idx, loop_state):
        a_local, tau_out, tfac_out = loop_state
        owner_col = panel_idx % col_count
        pivot_ids = panel_idx * block_width + col_ids
        panel_in = lax.dynamic_index_in_dim(a_local, panel_idx // col_count, axis=1, keepdims=False)
        panel_out, tau_vec = factor_panel_rows(panel_in, row_base, panel_idx * block_width, row_count)
        refl_mat = jnp.where(row_ids[:, None] > pivot_ids[None, :], panel_out, jnp.where(row_ids[:, None] == pivot_ids[None, :], 1.0, 0.0))
        gram_mat = axis_sum(mat_einsum('rk,rj->kj', refl_mat, refl_mat), 'row', row_count, 2)
        t_factor = tfactor_from_gram(gram_mat, tau_vec)
        packed = jnp.concatenate([refl_mat, t_factor], axis=0)
        packed = axis_sum(jnp.where(col_rank == owner_col, packed, 0.0), 'col', col_count, 3)
        refl_mat = packed[:local_rows]
        t_factor = packed[local_rows:]
        w_summed = axis_sum(mat_einsum('rk,rbc->kbc', refl_mat, a_local), 'row', row_count, 4)
        w_mat = mat_einsum('kj,kbc->jbc', t_factor, w_summed)
        w_mat = jnp.where((global_ids > panel_idx)[None, :, None], w_mat, 0.0)
        a_local = a_local - mat_einsum('rj,jbc->rbc', refl_mat, w_mat)
        a_local = jnp.where((global_ids == panel_idx)[None, :, None], panel_out[:, None, :], a_local)
        tau_out = lax.dynamic_update_index_in_dim(tau_out, jnp.diagonal(t_factor), panel_idx, 0)
        tfac_out = lax.dynamic_update_index_in_dim(tfac_out, t_factor, panel_idx, 0)
        return a_local, tau_out, tfac_out

    zero_tau = jnp.zeros((PANELS, block_width), jnp.float32)
    zero_tfac = jnp.zeros((PANELS, block_width, block_width), jnp.float32)
    a_local, tau_out, tfac_out = lax.fori_loop(0, PANELS, panel_step, (a_local, zero_tau, zero_tfac))
    return a_local, tau_out.reshape(-1), tfac_out


CHUNKS = 8
CROSS_ROWS = 256


def dot_nn(left_mat, right_mat):
    return lax.dot_general(left_mat, right_mat, (((1,), (0,)), ((), ())), precision=HIGHEST, preferred_element_type=jnp.float32)


def split3(mat):
    hi = mat.astype(jnp.bfloat16)
    rest = mat - hi.astype(jnp.float32)
    mid = rest.astype(jnp.bfloat16)
    return hi, mid, (rest - mid.astype(jnp.float32)).astype(jnp.bfloat16)


def bf_nn(left_mat, right_mat):
    return lax.dot_general(left_mat, right_mat, (((1,), (0,)), ((), ())), preferred_element_type=jnp.float32)


def bf_nt(left_mat, right_mat):
    return lax.dot_general(left_mat, right_mat, (((1,), (1,)), ((), ())), preferred_element_type=jnp.float32)


def dot_nt(left_mat, right_mat):
    return lax.dot_general(left_mat, right_mat, (((1,), (1,)), ((), ())), precision=HIGHEST, preferred_element_type=jnp.float32)


def factor_steps(w_ref, vinv_ref, rv_ref, u_ref):
    n = vinv_ref.shape[0]
    row_ids = lax.broadcasted_iota(jnp.int32, (n, n), 0)
    lane_ids = lax.broadcasted_iota(jnp.int32, (n, n), 1)
    line_ids = lax.broadcasted_iota(jnp.int32, (1, n), 1)

    def step(k, tau_line):
        g_line = w_ref[pl.ds(2 * n + k, 1), :]
        m_line = w_ref[pl.ds(k, 1), :]
        here = line_ids == k
        norm_sq = jnp.sum(jnp.where(here, g_line, 0.0), axis=1, keepdims=True)
        alpha = jnp.sum(jnp.where(here, m_line, 0.0), axis=1, keepdims=True)
        norm = jnp.sqrt(norm_sq)
        beta = jnp.where(alpha >= 0.0, -norm, norm)
        pivot = alpha - beta
        beta_rec = 1.0 / beta
        pivot_rec = 1.0 / pivot
        tau_line = jnp.where(here, (beta - alpha) * beta_rec, tau_line)
        r_line = jnp.where(here, beta, jnp.where(line_ids > k, g_line * beta_rec, 0.0))
        u_line = jnp.where(line_ids >= k, m_line - r_line, 0.0)
        u_ref[pl.ds(k, 1), :] = u_line
        v_line = vinv_ref[pl.ds(k, 1), :]
        u_tail = jnp.where(line_ids > k, u_line, 0.0)
        r_tail = jnp.where(line_ids > k, r_line, 0.0)
        at_col = lane_ids == k
        col_m = jnp.sum(jnp.where(at_col, w_ref[0:n], 0.0), axis=1, keepdims=True) * pivot_rec
        col_u = jnp.sum(jnp.where(at_col, w_ref[n:2 * n], 0.0), axis=1, keepdims=True) * pivot_rec
        col_g = jnp.sum(jnp.where(at_col, w_ref[2 * n:3 * n], 0.0), axis=1, keepdims=True) * beta_rec
        col_r = jnp.sum(jnp.where(at_col, w_ref[3 * n:4 * n], 0.0), axis=1, keepdims=True) * beta_rec
        col_m = jnp.where(row_ids[:, 0:1] > k, col_m, 0.0)
        col_g = jnp.where(row_ids[:, 0:1] > k, col_g, 0.0)
        rv_ref[...] = jnp.where(at_col & (row_ids > k), col_m, rv_ref[...])
        rv_ref[pl.ds(k, 1), :] = rv_ref[pl.ds(k, 1), :] + r_line
        w_ref[0:n] = w_ref[0:n] - col_m * u_tail
        w_ref[n:2 * n] = jnp.where(at_col, col_u, w_ref[n:2 * n] - col_u * u_tail)
        w_ref[2 * n:3 * n] = w_ref[2 * n:3 * n] - col_g * r_tail
        w_ref[3 * n:4 * n] = jnp.where(at_col, col_r, w_ref[3 * n:4 * n] - col_r * r_tail)
        vinv_ref[...] = vinv_ref[...] - col_m * v_line
        return tau_line

    return lax.fori_loop(0, n, step, jnp.zeros((1, n), jnp.float32))


def front_kernel(row_count, block_width, a_hbm, a_copy, vt_out, yt_out, rvt_out, tau_out, tf_out, flag_out,
                 a_buf, lead, ct_acc, g_acc, g_send, g_recv, g_part, g_all, c_recv, top_t, a11_t, yt_buf, max_buf,
                 w_ref, vinv_ref, rv_ref, u_ref,
                 own_sem, load_sem, keep_sem, right_send, left_send, fwd_send, from_left, from_right, fwd_recv,
                 max_send, max_recv, a11_send, a11_recv, top_send, top_recv,
                 gs_send, gs_recv, ga_send, ga_recv, cs_send, cs_recv, y_send, y_recv):
    local_cols, local_rows = a_hbm.shape
    n = PANELS * block_width
    chunk = local_rows // CHUNKS
    share = local_cols // row_count
    g_rows = n // row_count
    row_rank = lax.axis_index('row')
    col_rank = lax.axis_index('col')
    right_col, left_col, far_col = lax.rem(col_rank + 1, 4), lax.rem(col_rank + 3, 4), lax.rem(col_rank + 2, 4)

    def lanes(c):
        return pl.ds(pl.multiple_of(c * chunk, chunk), chunk)

    def panel(p):
        return pl.ds(pl.multiple_of(p * block_width, block_width), block_width)

    def peer_of(step):
        return lax.rem(row_rank + step, row_count)

    def own_copy(c):
        return pltpu.make_async_copy(a_hbm.at[0:block_width, lanes(c)], lead.at[panel(col_rank), lanes(c)], own_sem.at[c])

    def load_copy(c):
        return pltpu.make_async_copy(a_hbm.at[:, lanes(c)], a_buf.at[:, lanes(c)], load_sem.at[c])

    def keep_copy(c):
        return pltpu.make_async_copy(a_buf.at[:, lanes(c)], a_copy.at[:, lanes(c)], keep_sem.at[c])

    def to_col(c, owner, target, send_sem, recv_sem):
        return pltpu.make_async_remote_copy(
            src_ref=lead.at[panel(owner), lanes(c)], dst_ref=lead.at[panel(owner), lanes(c)],
            send_sem=send_sem.at[c], recv_sem=recv_sem.at[c], device_id={'col': target}, device_id_type=MESH)

    def to_row(src_ref, dst_ref, send_sem, recv_sem, target):
        return pltpu.make_async_remote_copy(
            src_ref=src_ref, dst_ref=dst_ref, send_sem=send_sem, recv_sem=recv_sem,
            device_id={'row': target}, device_id_type=MESH)

    def send_right(c):
        return to_col(c, col_rank, right_col, right_send, from_left)

    def send_left(c):
        return to_col(c, col_rank, left_col, left_send, from_right)

    @pl.loop(0, CHUNKS)
    def _(c):
        own_copy(c).start()

    @pl.loop(0, CHUNKS)
    def _(c):
        load_copy(c).start()

    barrier = pltpu.get_barrier_semaphore()
    for step in range(1, row_count):
        pl.semaphore_signal(barrier, inc=1, device_id={'row': peer_of(step)}, device_id_type=MESH)
    for step in range(1, 4):
        pl.semaphore_signal(barrier, inc=1, device_id={'col': lax.rem(col_rank + step, 4)}, device_id_type=MESH)
    pl.semaphore_wait(barrier, row_count - 1 + 3)

    def top_copy(target):
        return to_row(a_hbm.at[pl.ds(pl.multiple_of(target * share, share), share), 0:n], top_t, top_send.at[target], top_recv, target)

    def a11_copy(target):
        return to_row(lead.at[:, 0:n], a11_t, a11_send.at[target], a11_recv, target)

    for c in range(2):
        own_copy(c).wait()
        send_right(c).start()
        send_left(c).start()
    g_acc[...] = jnp.zeros_like(g_acc)
    ct_acc[...] = jnp.zeros_like(ct_acc)

    def cross_step(c):
        hi, mid, lo = split3(lead[:, lanes(c)])
        hi_mid = jnp.concatenate([hi, mid], axis=0)

        @pl.loop(0, local_cols // CROSS_ROWS)
        def _(i):
            at_rows = pl.ds(pl.multiple_of(i * CROSS_ROWS, CROSS_ROWS), CROSS_ROWS)
            a_hi, a_mid, a_lo = split3(a_buf[at_rows, lanes(c)])
            pair = bf_nt(a_mid, hi_mid) + bf_nt(a_hi, hi_mid)
            rest = bf_nt(a_lo, hi) + bf_nt(a_hi, lo)
            ct_acc[at_rows, :] = ct_acc[at_rows, :] + (pair[:, 0:n] + (pair[:, n:] + rest))

    def abs_max(c):
        part = jnp.abs(a_buf[:, lanes(c)])
        return jnp.max(jnp.max(part.reshape(local_cols // 8, 8, chunk), axis=0).reshape(8, chunk // 128, 128), axis=1)

    def max_copy(step):
        target = lax.rem(col_rank + step, 4)
        return pltpu.make_async_remote_copy(
            src_ref=max_buf.at[0], dst_ref=max_buf.at[step], send_sem=max_send.at[step], recv_sem=max_recv.at[step],
            device_id={'col': target}, device_id_type=MESH)

    max_buf[0] = jnp.zeros((8, 128), jnp.float32)

    @pl.loop(0, CHUNKS + 1)
    def _(c):
        @pl.when(c + 2 < CHUNKS)
        def _():
            own_copy(c + 2).wait()
            send_right(c + 2).start()
            send_left(c + 2).start()

        @pl.when(c < CHUNKS)
        def _():
            to_col(c, left_col, right_col, right_send, from_left).wait_recv()
            to_col(c, right_col, left_col, left_send, from_right).wait_recv()

            @pl.when(lax.rem(c, 2) == 0)
            def _():
                to_col(c, left_col, right_col, fwd_send, fwd_recv).start()

            @pl.when(lax.rem(c, 2) == 1)
            def _():
                to_col(c, right_col, left_col, fwd_send, fwd_recv).start()
            load_copy(c).wait()
            keep_copy(c).start()
            max_buf[0] = jnp.maximum(max_buf[0], abs_max(c))

        @pl.when(c > 0)
        def _():
            to_col(c - 1, far_col, right_col, fwd_send, fwd_recv).wait_recv()
            part = lead[:, lanes(c - 1)]
            g_acc[...] = g_acc[...] + dot_nt(part, part)

        @pl.when(c == 1)
        def _():
            @pl.when(row_rank == 0)
            def _():
                for target in range(1, row_count):
                    top_copy(target).start()
                    a11_copy(target).start()

        @pl.when(c == CHUNKS - 1)
        def _():
            for step in range(1, 4):
                max_copy(step).start()

        @pl.when(c > CHUNKS // 2)
        def _():
            cross_step(c - CHUNKS // 2 - 1)

    for step in range(1, 4):
        max_copy(step).wait_recv()
    big = jnp.maximum(jnp.maximum(max_buf[0], max_buf[1]), jnp.maximum(max_buf[2], max_buf[3]))
    for i in range(row_count):
        g_send[i, 0:g_rows] = g_acc[i * g_rows:(i + 1) * g_rows, :]
        g_send[i, g_rows:g_rows + 8] = big

    def gs_copy(step):
        return to_row(g_send.at[peer_of(step)], g_recv.at[row_rank], gs_send.at[step], gs_recv.at[step], peer_of(step))

    def ga_copy(step):
        return to_row(g_part, g_all.at[row_rank], ga_send.at[step], ga_recv.at[step], peer_of(step))

    def cs_copy(step):
        at_rows = pl.ds(pl.multiple_of(peer_of(step) * share, share), share)
        return to_row(ct_acc.at[at_rows, :], c_recv.at[row_rank], cs_send.at[step], cs_recv.at[step], peer_of(step))

    my_share = pl.ds(pl.multiple_of(row_rank * share, share), share)

    def y_copy(step):
        return to_row(yt_buf.at[my_share, :], yt_buf.at[my_share, :], y_send.at[step], y_recv.at[step], peer_of(step))

    def arrived(send_kind, buf, sems, step):
        source = lax.rem(row_rank + row_count - step, row_count)
        to_row(buf.at[source], buf.at[source], send_kind.at[step], sems.at[step], source).wait_recv()

    for step in range(1, row_count):
        gs_copy(step).start()
    g_recv[row_rank] = g_send[row_rank]

    @pl.loop(CHUNKS // 2, 3 * CHUNKS // 4)
    def _(c):
        cross_step(c)
    for step in range(1, row_count):
        arrived(gs_send, g_recv, gs_recv, step)
    total = g_recv[0, 0:g_rows]
    big = g_recv[0, g_rows:g_rows + 8]
    for i in range(1, row_count):
        total = total + g_recv[i, 0:g_rows]
        big = jnp.maximum(big, g_recv[i, g_rows:g_rows + 8])
    g_part[0:g_rows] = total
    g_part[g_rows:g_rows + 8] = big
    for step in range(1, row_count):
        ga_copy(step).start()
    g_all[row_rank] = g_part[...]

    @pl.loop(3 * CHUNKS // 4, CHUNKS)
    def _(c):
        cross_step(c)
    for step in range(1, row_count):
        cs_copy(step).start()
    c_recv[row_rank] = ct_acc[my_share, :]
    for step in range(1, row_count):
        arrived(ga_send, g_all, ga_recv, step)

    @pl.when(row_rank == 0)
    def _():
        a11_t[...] = lead[:, 0:n]
        top_t[...] = a_buf[0:share, 0:n]

    @pl.when(row_rank > 0)
    def _():
        a11_copy(row_rank).wait_recv()
        top_copy(row_rank).wait_recv()

    row_ids = lax.broadcasted_iota(jnp.int32, (n, n), 0)
    lane_ids = lax.broadcasted_iota(jnp.int32, (n, n), 1)
    eye = jnp.where(row_ids == lane_ids, 1.0, 0.0)
    big = g_all[0, g_rows:g_rows + 8]
    for i in range(row_count):
        g_acc[i * g_rows:(i + 1) * g_rows, :] = g_all[i, 0:g_rows]
        big = jnp.maximum(big, g_all[i, g_rows:g_rows + 8])
    w_ref[0:n] = a11_t[...].T
    w_ref[n:2 * n] = eye
    w_ref[2 * n:3 * n] = g_acc[...]
    w_ref[3 * n:4 * n] = eye
    vinv_ref[...] = eye
    rv_ref[...] = jnp.zeros((n, n), jnp.float32)
    u_ref[...] = jnp.zeros((n, n), jnp.float32)
    tau_out[...] = factor_steps(w_ref, vinv_ref, rv_ref, u_ref)
    u_inv = w_ref[n:2 * n]
    r_inv = w_ref[3 * n:4 * n]

    for step in range(1, row_count):
        arrived(cs_send, c_recv, cs_recv, step)
    cross = c_recv[0]
    for i in range(1, row_count):
        cross = cross + c_recv[i]
    yt_buf[my_share, :] = dot_nt(top_t[...] - dot_nn(cross, r_inv), vinv_ref[...])
    for step in range(1, row_count):
        y_copy(step).start()

    diag = jnp.sum(jnp.where(row_ids == lane_ids, g_acc[...], 0.0), axis=1, keepdims=True)
    cond_val = jnp.sum(jnp.sum(diag * r_inv * r_inv, axis=1, keepdims=True), axis=0, keepdims=True)
    big_val = jnp.max(jnp.max(big, axis=1, keepdims=True), axis=0, keepdims=True)
    low_val = jnp.min(diag, axis=0, keepdims=True)
    usable = (cond_val < COND_MAX) & (big_val < ABS_MAX) & (low_val > GRAM_MIN)
    flag_out[...] = jnp.broadcast_to(jnp.where(usable, 1.0, 0.0), (8, 128))
    tf_out[...] = -dot_nn(u_ref[...], dot_nt(r_inv, vinv_ref[...]))
    rv_t = rv_ref[...].T
    rvt_out[...] = rv_t
    u_inv_t = u_inv.T

    @pl.loop(0, CHUNKS)
    def _(c):
        vt_out[:, lanes(c)] = dot_nn(u_inv_t, lead[:, lanes(c)])

    @pl.when(row_rank == 0)
    def _():
        vt_out[:, 0:n] = jnp.where(lane_ids > row_ids, rv_t, eye)

    for step in range(1, row_count):
        source = lax.rem(row_rank + row_count - step, row_count)
        at_rows = pl.ds(pl.multiple_of(source * share, share), share)
        to_row(yt_buf.at[at_rows, :], yt_buf.at[at_rows, :], y_send.at[step], y_recv.at[step], source).wait_recv()
    yt_out[...] = yt_buf[...]

    @pl.loop(0, CHUNKS)
    def _(c):
        send_right(c).wait_send()
        send_left(c).wait_send()
        to_col(c, left_col, right_col, fwd_send, fwd_recv).wait_send()
        keep_copy(c).wait()
    for step in range(1, 4):
        max_copy(step).wait_send()
    for step in range(1, row_count):
        gs_copy(step).wait_send()
        ga_copy(step).wait_send()
        cs_copy(step).wait_send()
        y_copy(step).wait_send()

    @pl.when(row_rank == 0)
    def _():
        for target in range(1, row_count):
            top_copy(target).wait_send()
            a11_copy(target).wait_send()


def front(a_t, row_count, block_width):
    local_cols, local_rows = a_t.shape
    n = PANELS * block_width
    share = local_cols // row_count
    g_rows = n // row_count
    f32 = jnp.float32
    mat = jax.ShapeDtypeStruct((n, n), f32)
    vmem, sem = pltpu.VMEM, pltpu.SemaphoreType.DMA
    spec = pl.BlockSpec(memory_space=pltpu.VMEM)
    return pl.pallas_call(
        functools.partial(front_kernel, row_count, block_width),
        out_shape=(jax.ShapeDtypeStruct(a_t.shape, f32), jax.ShapeDtypeStruct((n, local_rows), f32), jax.ShapeDtypeStruct((local_cols, n), f32), mat,
                   jax.ShapeDtypeStruct((1, n), f32), mat, jax.ShapeDtypeStruct((8, 128), f32)),
        in_specs=[pl.BlockSpec(memory_space=pl.ANY)],
        out_specs=[pl.BlockSpec(memory_space=pl.ANY)] + [spec] * 6,
        scratch_shapes=[
            vmem((local_cols, local_rows), f32), vmem((n, local_rows), f32), vmem((local_cols, n), f32), vmem((n, n), f32),
            vmem((row_count, g_rows + 8, n), f32), vmem((row_count, g_rows + 8, n), f32), vmem((g_rows + 8, n), f32),
            vmem((row_count, g_rows + 8, n), f32), vmem((row_count, share, n), f32), vmem((share, n), f32), vmem((n, n), f32),
            vmem((local_cols, n), f32), vmem((4, 8, 128), f32),
            vmem((4 * n, n), f32), vmem((n, n), f32), vmem((n, n), f32), vmem((n, n), f32),
            sem((CHUNKS,)), sem((CHUNKS,)), sem((CHUNKS,)), sem((CHUNKS,)), sem((CHUNKS,)), sem((CHUNKS,)), sem((CHUNKS,)), sem((CHUNKS,)), sem((CHUNKS,)),
            sem((4,)), sem((4,)), sem((row_count,)), sem, sem((row_count,)), sem,
            sem((row_count,)), sem((row_count,)), sem((row_count,)), sem((row_count,)),
            sem((row_count,)), sem((row_count,)), sem((row_count,)), sem((row_count,)),
        ],
        compiler_params=pltpu.CompilerParams(collective_id=0, has_side_effects=True, vmem_limit_bytes=60 * 1024 * 1024),
        name='front',
    )(a_t)


def update_kernel(block_width, a_ref, vt_ref, yt_ref, rvt_ref, out_ref, y_hm, y_hl):
    n = vt_ref.shape[0]
    local_cols = a_ref.shape[0]
    step_rows = 256
    own = pl.ds(pl.multiple_of(lax.axis_index('col') * block_width, block_width), block_width)

    def rows_of(i):
        return pl.ds(pl.multiple_of(i * step_rows, step_rows), step_rows)

    @pl.when(pl.program_id(0) == 0)
    def _():
        @pl.loop(0, local_cols // step_rows)
        def _(i):
            hi, mid, lo = split3(yt_ref[rows_of(i), :])
            y_hm[rows_of(i), :] = jnp.concatenate([hi, mid], axis=1)
            y_hl[rows_of(i), :] = jnp.concatenate([hi, lo], axis=1)

    hi, mid, lo = split3(vt_ref[...])
    hi_hi = jnp.concatenate([hi, hi], axis=0)
    mid_mid = jnp.concatenate([mid, mid], axis=0)
    lo_hi = jnp.concatenate([lo, hi], axis=0)

    @pl.loop(0, local_cols // step_rows)
    def _(i):
        left = y_hm[rows_of(i), :]
        prod = (bf_nn(y_hl[rows_of(i), :], lo_hi) + bf_nn(left, mid_mid)) + bf_nn(left, hi_hi)
        out_ref[rows_of(i), :] = a_ref[rows_of(i), :] - prod
    out_ref[0:block_width, :] = vt_ref[own, :]

    @pl.when((lax.axis_index('row') == 0) & (pl.program_id(0) == 0))
    def _():
        out_ref[0:block_width, 0:n] = rvt_ref[own, :]


def update(a_t, vt, yt, rvt, block_width, tile=512):
    local_cols, local_rows = a_t.shape
    n = vt.shape[0]
    return pl.pallas_call(
        functools.partial(update_kernel, block_width),
        out_shape=jax.ShapeDtypeStruct(a_t.shape, jnp.float32),
        grid=(local_rows // tile,),
        in_specs=[pl.BlockSpec((local_cols, tile), lambda i: (0, i)), pl.BlockSpec((n, tile), lambda i: (0, i)),
                  pl.BlockSpec((local_cols, n), lambda i: (0, 0)), pl.BlockSpec((n, n), lambda i: (0, 0))],
        out_specs=pl.BlockSpec((local_cols, tile), lambda i: (0, i)),
        scratch_shapes=[pltpu.VMEM((local_cols, 2 * n), jnp.bfloat16)] * 2,
        compiler_params=pltpu.CompilerParams(dimension_semantics=('arbitrary',), vmem_limit_bytes=56 * 1024 * 1024),
        name='update',
    )(a_t, vt, yt, rvt)


def solution(mesh):
    col_count = mesh.shape['col']
    row_count = mesh.shape['row']
    assert col_count == PANELS == 4
    block_spec = P(('batch', 'row'), 'col', None)

    def device_fn(a_local):
        local_rows, local_blocks, block_width = a_local.shape
        width = PANELS * block_width
        local_cols = local_blocks * block_width
        a_t = a_local.transpose(1, 2, 0).reshape(local_cols, local_rows)
        kept, vt, yt, rvt, tau_line, t_full, flag = front(a_t, row_count, block_width)
        out_t = update(a_t, vt, yt, rvt, block_width)
        tfac = jnp.stack([t_full[s:s + block_width, s:s + block_width] for s in range(0, width, block_width)])

        def column_form(state):
            kept = state[4]
            a_local = kept.reshape(local_blocks, block_width, local_rows).transpose(2, 0, 1)
            a_out, tau, tfac = columnwise_qr(a_local, col_count, row_count)
            return jnp.int32(0), a_out.transpose(1, 2, 0).reshape(local_cols, local_rows), tau, tfac, kept

        redo = jnp.where(flag[0, 0] > 0.5, 0, 1).astype(jnp.int32)
        state = (redo, out_t, tau_line[0], tfac, kept)
        _, out_t, tau, tfac, _ = lax.while_loop(lambda state: state[0] > 0, column_form, state)
        return out_t.reshape(local_blocks, block_width, local_rows).transpose(2, 0, 1), tau, tfac

    return jax.shard_map(device_fn, mesh=mesh, in_specs=(block_spec,), out_specs=(block_spec, P('batch'), P('batch', None, None)), check_vma=False)
```

time: 3180 us -> 101 us (0.03)
  blocking collectives: 1690 us -> 0 us
  waiting for transfers between devices: 372 us -> 0 us
  loops' own time: 361 us -> 0.01 us
  matrix products: 307 us -> 0 us
  other arithmetic: 224 us -> 0.64 us
  local copies, waits for them, and re-layouts: 192 us -> 3.21 us
  Pallas kernels: 0 us -> 95.5 us
    psum x132 -> x0, blocking collectives: 1690 us -> none  [the longest x128 1610 us: column_step(): packed = lax.psum(packed, 'row')]
    psum x8 -> x0, waiting for transfers between devices: 372 us -> none  [the longest x4 223 us: device_fn(): w_summed = lax.psum(mat_einsum('rk,rbc->kbc', refl_mat, a_local), 'row')]
    another operation x4 -> x1, loops' own time: 361 us -> 0.01 us  [device_fn(): lax.while_loop(lambda state: state[0] > 0, column_form, state)]
    dot_general x172 -> x0, matrix products: 245 us -> none  [the longest x12 174 us: mat_einsum(): jnp.einsum(einsum_form, left_mat, right_mat, precision=HIGHEST, preferred...]
    select_n x652 -> x0, other arithmetic: 209 us -> none  [the longest x128 95.3 us: apply_reflector(): refl_dot = jnp.where(col_ids > col_idx, refl_dot, 0.0)]
    dynamic_slice x384 -> x0, local copies, waits for them, and re-layouts: 157 us -> none  [the longest x128 80.5 us: apply_reflector(): alpha_val = lax.dynamic_index_in_dim(pivot_line, col_idx, keepdims=False)]
    pallas_call x0 -> x2, Pallas kernels: none -> 95.5 us  [the longest x1 76.8 us: front(): pl.pallas_call(functools.partial(front_kernel, row_count, block_width), o...]
    unnamed x4 -> x0, matrix products: 61.8 us -> none
  transfers between devices with their start and end apart: 8 -> 0, of which waited for: 8 -> 0; matrix products, arithmetic and copies ran while one was open for 0% -> 0% of each run, Pallas kernels for 0% -> 0%
where the time goes in v1:
time: 101 us
  Pallas kernels  95.5 us (95%)
  local copies, waits for them, and re-layouts  3.21 us (3%)
  between operations  1.3 us (1%)
    pallas_call x1, Pallas kernels, front(): pl.pallas_call(functools.partial(front_kernel, row_count, block_width), o...  76.8 us
    pallas_call x1, Pallas kernels, update(): pl.pallas_call(functools.partial(update_kernel, block_width), out_shape=j...  18.7 us

profile of v1, /device:TPU:97, one launch (start us, length us, event | category | flops | bytes accessed | tf_op | source)
XLA Modules:
  0.0 100.7 jit_solution(10558287539235282603)
XLA Ops:
  0.6 76.8 %front.1 = (f32[1024,4096]{1,0:T(8,128)}, f32[128,4096]{1,0:T(8,128)}, f32[1024,128]{1,0:T(8,128)}, f32[128,128]{1,0:T(8,128)}, f32[1,128]{1,0:T(1,128)}, /*index=5*/f32[128,128]{1,0:T(8,128)}, f32[8,128]{1,0:T(8,128)}) custom-call(f32[1024,4096]{1,0:T(8,128)} %bitcast.153), custom_call_target="tpu_custom_call" | custom-call | tf_op jit(solution)/shard_map/front/pallas_call | solution.py:518
  77.4 1.2 %slice.66 = f32[1,1]{1,0:T(1,128)} slice(f32[8,128]{1,0:T(8,128)} %get-tuple-element.486), slice={[0:1], [0:1]} | slice | bytes 8 | tf_op jit(solution)/shard_map/slice | solution.py:611
  79.3 0.8 slice_bitcast_fusion.3
  80.1 0.6 pad_maximum_fusion
  80.8 18.7 %update.1 = f32[1024,4096]{1,0:T(8,128)} custom-call(f32[1024,4096]{1,0:T(8,128)} %bitcast.154, f32[128,4096]{1,0:T(8,128)} %get-tuple-element.487.vt_ref, f32[1024,128]{1,0:T(8,128)} %get-tuple-element.488.yt_ref, f32[128,128]{1,0:T(8,128)} %get-tuple-element.489.rvt_ref), custom_call_target="tpu_custom_call" | custom-call | tf_op jit(solution)/shard_map/update/pallas_call | solution.py:577
  99.5 1.2 %copy.71 = f32[128]{0:T(128)} copy(f32[128]{0:T(128)} %get-tuple-element.904) | data formatting | bytes 1024
  (1 shorter events, 0.0 us)

commit v2 on v1

--- a/solution.py
+++ b/solution.py
@@ -150,8 +150,10 @@
     return a_local, tau_out.reshape(-1), tfac_out
 
 
-CHUNKS = 8
-CROSS_ROWS = 256
+CHUNKS = 4
+CROSS_ROWS = 512
+SUB = 4
+ROWS = 512
 
 
 def dot_nn(left_mat, right_mat):
@@ -177,52 +179,81 @@
     return lax.dot_general(left_mat, right_mat, (((1,), (1,)), ((), ())), precision=HIGHEST, preferred_element_type=jnp.float32)
 
 
-def factor_steps(w_ref, vinv_ref, rv_ref, u_ref):
+def factor_steps(w1_ref, w2_ref, vinv_ref, v_ref, r_ref, u_ref):
     n = vinv_ref.shape[0]
-    row_ids = lax.broadcasted_iota(jnp.int32, (n, n), 0)
+    row_col = lax.broadcasted_iota(jnp.int32, (n, 1), 0)
     lane_ids = lax.broadcasted_iota(jnp.int32, (n, n), 1)
+    lane8 = lax.broadcasted_iota(jnp.int32, (8, n), 1)
+    sub_col = lax.broadcasted_iota(jnp.int32, (8, 1), 0)
     line_ids = lax.broadcasted_iota(jnp.int32, (1, n), 1)
 
-    def step(k, tau_line):
-        g_line = w_ref[pl.ds(2 * n + k, 1), :]
-        m_line = w_ref[pl.ds(k, 1), :]
-        here = line_ids == k
-        norm_sq = jnp.sum(jnp.where(here, g_line, 0.0), axis=1, keepdims=True)
-        alpha = jnp.sum(jnp.where(here, m_line, 0.0), axis=1, keepdims=True)
-        norm = jnp.sqrt(norm_sq)
-        beta = jnp.where(alpha >= 0.0, -norm, norm)
-        pivot = alpha - beta
-        beta_rec = 1.0 / beta
-        pivot_rec = 1.0 / pivot
-        tau_line = jnp.where(here, (beta - alpha) * beta_rec, tau_line)
-        r_line = jnp.where(here, beta, jnp.where(line_ids > k, g_line * beta_rec, 0.0))
-        u_line = jnp.where(line_ids >= k, m_line - r_line, 0.0)
-        u_ref[pl.ds(k, 1), :] = u_line
-        v_line = vinv_ref[pl.ds(k, 1), :]
-        u_tail = jnp.where(line_ids > k, u_line, 0.0)
-        r_tail = jnp.where(line_ids > k, r_line, 0.0)
-        at_col = lane_ids == k
-        col_m = jnp.sum(jnp.where(at_col, w_ref[0:n], 0.0), axis=1, keepdims=True) * pivot_rec
-        col_u = jnp.sum(jnp.where(at_col, w_ref[n:2 * n], 0.0), axis=1, keepdims=True) * pivot_rec
-        col_g = jnp.sum(jnp.where(at_col, w_ref[2 * n:3 * n], 0.0), axis=1, keepdims=True) * beta_rec
-        col_r = jnp.sum(jnp.where(at_col, w_ref[3 * n:4 * n], 0.0), axis=1, keepdims=True) * beta_rec
-        col_m = jnp.where(row_ids[:, 0:1] > k, col_m, 0.0)
-        col_g = jnp.where(row_ids[:, 0:1] > k, col_g, 0.0)
-        rv_ref[...] = jnp.where(at_col & (row_ids > k), col_m, rv_ref[...])
-        rv_ref[pl.ds(k, 1), :] = rv_ref[pl.ds(k, 1), :] + r_line
-        w_ref[0:n] = w_ref[0:n] - col_m * u_tail
-        w_ref[n:2 * n] = jnp.where(at_col, col_u, w_ref[n:2 * n] - col_u * u_tail)
-        w_ref[2 * n:3 * n] = w_ref[2 * n:3 * n] - col_g * r_tail
-        w_ref[3 * n:4 * n] = jnp.where(at_col, col_r, w_ref[3 * n:4 * n] - col_r * r_tail)
-        vinv_ref[...] = vinv_ref[...] - col_m * v_line
+    def pick(mask, mat):
+        return jnp.sum(jnp.where(mask, mat, 0.0), axis=1, keepdims=True)
+
+    def step(b, tau_line):
+        base = pl.multiple_of(b * 8, 8)
+        rows8 = pl.ds(base, 8)
+        for first in range(0, 8, SUB):
+            tile1, tile2 = w1_ref[rows8, :], w2_ref[rows8, :]
+            ks = [base + first + j for j in range(SUB)]
+            d1 = [pick(lane8 == k, tile1) for k in ks]
+            d2 = [pick(lane8 == k, tile2) for k in ks]
+            w1, w2 = w1_ref[...], w2_ref[...]
+            c1 = [pick(lane_ids == k, w1) for k in ks]
+            c2 = [pick(lane_ids == k, w2) for k in ks]
+            below = row_col >= base + 8
+            v_mat = v_ref[...]
+            for j in range(SUB):
+                at, k = first + j, ks[j]
+                alpha, norm_sq = d1[j][at:at + 1], d2[j][at:at + 1]
+                norm = jnp.sqrt(norm_sq)
+                beta = jnp.where(alpha >= 0.0, -norm, norm)
+                beta_rec = 1.0 / beta
+                pivot_rec = 1.0 / (alpha - beta)
+                line1, line2 = tile1[at:at + 1, :], tile2[at:at + 1, :]
+                here, after = line_ids == k, line_ids > k
+                tau_line = jnp.where(here, (beta - alpha) * beta_rec, tau_line)
+                r_tail = jnp.where(after, line2 * beta_rec, 0.0)
+                u_tail = jnp.where(after, line1 - r_tail, 0.0)
+                low = jnp.where(line_ids < k, line1, 0.0)
+                r_ref[pl.ds(k, 1), :] = jnp.where(here, beta, r_tail)
+                u_ref[pl.ds(k, 1), :] = jnp.where(here, alpha - beta, u_tail)
+                vinv_ref[pl.ds(k, 1), :] = jnp.where(here, 1.0, low)
+                m1 = jnp.where(sub_col == at, pivot_rec, d1[j] * pivot_rec)
+                m2 = jnp.where(sub_col == at, beta_rec, d2[j] * beta_rec)
+                f1, f2 = c1[j] * pivot_rec, c2[j] * beta_rec
+                for t in range(j + 1, SUB):
+                    r_val = d2[t][at:at + 1] * beta_rec
+                    u_val = d1[t][at:at + 1] - r_val
+                    d1[t] = jnp.where(sub_col == at, 0.0, d1[t]) - m1 * u_val
+                    d2[t] = jnp.where(sub_col == at, 0.0, d2[t]) - m2 * r_val
+                    c1[t] = c1[t] - f1 * u_val
+                    c2[t] = c2[t] - f2 * r_val
+                here8 = lane8 == k
+                rest8 = sub_col > at
+                tile1 = jnp.where(here8, jnp.where(rest8, -m1, m1),
+                                  jnp.where(sub_col == at, 0.0, tile1) - m1 * jnp.where(rest8, u_tail + low, u_tail))
+                tile2 = jnp.where(here8, m2, jnp.where(sub_col == at, 0.0, tile2) - m2 * r_tail)
+                v8 = jnp.where(rest8, m1, 0.0)
+                at_col = lane_ids == k
+                w1 = jnp.where(at_col, jnp.where(below, -f1, f1), w1 - f1 * jnp.where(below, u_tail + low, u_tail))
+                w2 = jnp.where(at_col, f2, w2 - f2 * r_tail)
+                v_mat = jnp.where(at_col, f1, v_mat)
+                v_rows = jnp.where(here8, v8, v_ref[rows8, :] if j == 0 else v_rows)
+            w1_ref[...] = w1
+            w2_ref[...] = w2
+            v_ref[...] = v_mat
+            w1_ref[rows8, :] = tile1
+            w2_ref[rows8, :] = tile2
+            v_ref[rows8, :] = v_rows
         return tau_line
 
-    return lax.fori_loop(0, n, step, jnp.zeros((1, n), jnp.float32))
+    return lax.fori_loop(0, n // 8, step, jnp.zeros((1, n), jnp.float32))
 
 
 def front_kernel(row_count, block_width, a_hbm, a_copy, vt_out, yt_out, rvt_out, tau_out, tf_out, flag_out,
                  a_buf, lead, ct_acc, g_acc, g_send, g_recv, g_part, g_all, c_recv, top_t, a11_t, yt_buf, max_buf,
-                 w_ref, vinv_ref, rv_ref, u_ref,
+                 w1_ref, w2_ref, vinv_ref, v_ref, r_ref, u_ref,
                  own_sem, load_sem, keep_sem, right_send, left_send, fwd_send, from_left, from_right, fwd_recv,
                  max_send, max_recv, a11_send, a11_recv, top_send, top_recv,
                  gs_send, gs_recv, ga_send, ga_recv, cs_send, cs_recv, y_send, y_recv):
@@ -300,13 +331,15 @@
     def cross_step(c):
         hi, mid, lo = split3(lead[:, lanes(c)])
         hi_mid = jnp.concatenate([hi, mid], axis=0)
+        hi_mid = jnp.concatenate([hi_mid, hi_mid], axis=1)
+        hi_lo = jnp.concatenate([hi, lo], axis=1)
 
         @pl.loop(0, local_cols // CROSS_ROWS)
         def _(i):
             at_rows = pl.ds(pl.multiple_of(i * CROSS_ROWS, CROSS_ROWS), CROSS_ROWS)
             a_hi, a_mid, a_lo = split3(a_buf[at_rows, lanes(c)])
-            pair = bf_nt(a_mid, hi_mid) + bf_nt(a_hi, hi_mid)
-            rest = bf_nt(a_lo, hi) + bf_nt(a_hi, lo)
+            pair = bf_nt(jnp.concatenate([a_mid, a_hi], axis=1), hi_mid)
+            rest = bf_nt(jnp.concatenate([a_lo, a_hi], axis=1), hi_lo)
             ct_acc[at_rows, :] = ct_acc[at_rows, :] + (pair[:, 0:n] + (pair[:, n:] + rest))
 
     def abs_max(c):
@@ -364,9 +397,9 @@
             for step in range(1, 4):
                 max_copy(step).start()
 
-        @pl.when(c > CHUNKS // 2)
+        @pl.when((c > 0) & (c < CHUNKS))
         def _():
-            cross_step(c - CHUNKS // 2 - 1)
+            cross_step(c - 1)
 
     for step in range(1, 4):
         max_copy(step).wait_recv()
@@ -387,8 +420,21 @@
 
     my_share = pl.ds(pl.multiple_of(row_rank * share, share), share)
 
+    partner = row_rank + 1 - 2 * lax.rem(row_rank, 2)
+
+    def y_rows(owner):
+        return pl.ds(pl.multiple_of(owner * share, share), share)
+
     def y_copy(step):
-        return to_row(yt_buf.at[my_share, :], yt_buf.at[my_share, :], y_send.at[step], y_recv.at[step], peer_of(step))
+        target = partner if step == 0 else peer_of(step)
+        return to_row(yt_buf.at[my_share, :], yt_buf.at[my_share, :], y_send.at[step], y_recv.at[step], target)
+
+    def y_pass(step):
+        source = lax.rem(row_rank + row_count - step, row_count)
+        return to_row(yt_buf.at[y_rows(source), :], yt_buf.at[y_rows(source), :], y_send.at[step + 1], y_recv.at[step + 1], partner)
+
+    def y_arrive(owner, slot):
+        to_row(yt_buf.at[y_rows(owner), :], yt_buf.at[y_rows(owner), :], y_send.at[slot], y_recv.at[slot], partner).wait_recv()
 
     def arrived(send_kind, buf, sems, step):
         source = lax.rem(row_rank + row_count - step, row_count)
@@ -398,9 +444,7 @@
         gs_copy(step).start()
     g_recv[row_rank] = g_send[row_rank]
 
-    @pl.loop(CHUNKS // 2, 3 * CHUNKS // 4)
-    def _(c):
-        cross_step(c)
+    cross_step(CHUNKS - 1)
     for step in range(1, row_count):
         arrived(gs_send, g_recv, gs_recv, step)
     total = g_recv[0, 0:g_rows]
@@ -414,9 +458,6 @@
         ga_copy(step).start()
     g_all[row_rank] = g_part[...]
 
-    @pl.loop(3 * CHUNKS // 4, CHUNKS)
-    def _(c):
-        cross_step(c)
     for step in range(1, row_count):
         cs_copy(step).start()
     c_recv[row_rank] = ct_acc[my_share, :]
@@ -440,16 +481,12 @@
     for i in range(row_count):
         g_acc[i * g_rows:(i + 1) * g_rows, :] = g_all[i, 0:g_rows]
         big = jnp.maximum(big, g_all[i, g_rows:g_rows + 8])
-    w_ref[0:n] = a11_t[...].T
-    w_ref[n:2 * n] = eye
-    w_ref[2 * n:3 * n] = g_acc[...]
-    w_ref[3 * n:4 * n] = eye
-    vinv_ref[...] = eye
-    rv_ref[...] = jnp.zeros((n, n), jnp.float32)
-    u_ref[...] = jnp.zeros((n, n), jnp.float32)
-    tau_out[...] = factor_steps(w_ref, vinv_ref, rv_ref, u_ref)
-    u_inv = w_ref[n:2 * n]
-    r_inv = w_ref[3 * n:4 * n]
+    w1_ref[...] = a11_t[...].T
+    w2_ref[...] = g_acc[...]
+    v_ref[...] = jnp.zeros((n, n), jnp.float32)
+    tau_out[...] = factor_steps(w1_ref, w2_ref, vinv_ref, v_ref, r_ref, u_ref)
+    u_inv = w1_ref[...]
+    r_inv = w2_ref[...]
 
     for step in range(1, row_count):
         arrived(cs_send, c_recv, cs_recv, step)
@@ -457,7 +494,7 @@
     for i in range(1, row_count):
         cross = cross + c_recv[i]
     yt_buf[my_share, :] = dot_nt(top_t[...] - dot_nn(cross, r_inv), vinv_ref[...])
-    for step in range(1, row_count):
+    for step in range(0, row_count, 2):
         y_copy(step).start()
 
     diag = jnp.sum(jnp.where(row_ids == lane_ids, g_acc[...], 0.0), axis=1, keepdims=True)
@@ -465,9 +502,11 @@
     big_val = jnp.max(jnp.max(big, axis=1, keepdims=True), axis=0, keepdims=True)
     low_val = jnp.min(diag, axis=0, keepdims=True)
     usable = (cond_val < COND_MAX) & (big_val < ABS_MAX) & (low_val > GRAM_MIN)
-    flag_out[...] = jnp.broadcast_to(jnp.where(usable, 1.0, 0.0), (8, 128))
-    tf_out[...] = -dot_nn(u_ref[...], dot_nt(r_inv, vinv_ref[...]))
-    rv_t = rv_ref[...].T
+    flag_out[0, 0] = jnp.max(jnp.where(usable, 0, 1))
+    t_full = -dot_nn(u_ref[...], dot_nt(r_inv, vinv_ref[...]))
+    for p in range(PANELS):
+        tf_out[p] = t_full[p * block_width:(p + 1) * block_width, p * block_width:(p + 1) * block_width]
+    rv_t = jnp.where(lane_ids < row_ids, v_ref[...], r_ref[...]).T
     rvt_out[...] = rv_t
     u_inv_t = u_inv.T
 
@@ -479,10 +518,12 @@
     def _():
         vt_out[:, 0:n] = jnp.where(lane_ids > row_ids, rv_t, eye)
 
-    for step in range(1, row_count):
-        source = lax.rem(row_rank + row_count - step, row_count)
-        at_rows = pl.ds(pl.multiple_of(source * share, share), share)
-        to_row(yt_buf.at[at_rows, :], yt_buf.at[at_rows, :], y_send.at[step], y_recv.at[step], source).wait_recv()
+    for step in range(2, row_count, 2):
+        y_arrive(lax.rem(row_rank + row_count - step, row_count), step)
+        y_pass(step).start()
+    y_arrive(partner, 0)
+    for step in range(2, row_count, 2):
+        y_arrive(lax.rem(partner + row_count - step, row_count), step + 1)
     yt_out[...] = yt_buf[...]
 
     @pl.loop(0, CHUNKS)
@@ -497,7 +538,10 @@
         gs_copy(step).wait_send()
         ga_copy(step).wait_send()
         cs_copy(step).wait_send()
+    y_copy(0).wait_send()
+    for step in range(2, row_count, 2):
         y_copy(step).wait_send()
+        y_pass(step).wait_send()
 
     @pl.when(row_rank == 0)
     def _():
@@ -518,15 +562,16 @@
     return pl.pallas_call(
         functools.partial(front_kernel, row_count, block_width),
         out_shape=(jax.ShapeDtypeStruct(a_t.shape, f32), jax.ShapeDtypeStruct((n, local_rows), f32), jax.ShapeDtypeStruct((local_cols, n), f32), mat,
-                   jax.ShapeDtypeStruct((1, n), f32), mat, jax.ShapeDtypeStruct((8, 128), f32)),
+                   jax.ShapeDtypeStruct((1, n), f32), jax.ShapeDtypeStruct((PANELS, block_width, block_width), f32),
+                   jax.ShapeDtypeStruct((1, 1), jnp.int32)),
         in_specs=[pl.BlockSpec(memory_space=pl.ANY)],
-        out_specs=[pl.BlockSpec(memory_space=pl.ANY)] + [spec] * 6,
+        out_specs=[pl.BlockSpec(memory_space=pl.ANY)] + [spec] * 5 + [pl.BlockSpec(memory_space=pltpu.SMEM)],
         scratch_shapes=[
             vmem((local_cols, local_rows), f32), vmem((n, local_rows), f32), vmem((local_cols, n), f32), vmem((n, n), f32),
             vmem((row_count, g_rows + 8, n), f32), vmem((row_count, g_rows + 8, n), f32), vmem((g_rows + 8, n), f32),
             vmem((row_count, g_rows + 8, n), f32), vmem((row_count, share, n), f32), vmem((share, n), f32), vmem((n, n), f32),
             vmem((local_cols, n), f32), vmem((4, 8, 128), f32),
-            vmem((4 * n, n), f32), vmem((n, n), f32), vmem((n, n), f32), vmem((n, n), f32),
+            vmem((n, n), f32), vmem((n, n), f32), vmem((n, n), f32), vmem((n, n), f32), vmem((n, n), f32), vmem((n, n), f32),
             sem((CHUNKS,)), sem((CHUNKS,)), sem((CHUNKS,)), sem((CHUNKS,)), sem((CHUNKS,)), sem((CHUNKS,)), sem((CHUNKS,)), sem((CHUNKS,)), sem((CHUNKS,)),
             sem((4,)), sem((4,)), sem((row_count,)), sem, sem((row_count,)), sem,
             sem((row_count,)), sem((row_count,)), sem((row_count,)), sem((row_count,)),
@@ -537,33 +582,25 @@
     )(a_t)
 
 
-def update_kernel(block_width, a_ref, vt_ref, yt_ref, rvt_ref, out_ref, y_hm, y_hl):
-    n = vt_ref.shape[0]
+def update_kernel(block_width, a_ref, vt_ref, yt_ref, rvt_ref, tau_ref, tf_ref, out_ref, tau_out, tf_out, y_parts):
+    n, tile = vt_ref.shape
     local_cols = a_ref.shape[0]
-    step_rows = 256
     own = pl.ds(pl.multiple_of(lax.axis_index('col') * block_width, block_width), block_width)
-
-    def rows_of(i):
-        return pl.ds(pl.multiple_of(i * step_rows, step_rows), step_rows)
 
     @pl.when(pl.program_id(0) == 0)
     def _():
-        @pl.loop(0, local_cols // step_rows)
-        def _(i):
-            hi, mid, lo = split3(yt_ref[rows_of(i), :])
-            y_hm[rows_of(i), :] = jnp.concatenate([hi, mid], axis=1)
-            y_hl[rows_of(i), :] = jnp.concatenate([hi, lo], axis=1)
-
-    hi, mid, lo = split3(vt_ref[...])
-    hi_hi = jnp.concatenate([hi, hi], axis=0)
-    mid_mid = jnp.concatenate([mid, mid], axis=0)
-    lo_hi = jnp.concatenate([lo, hi], axis=0)
-
-    @pl.loop(0, local_cols // step_rows)
-    def _(i):
-        left = y_hm[rows_of(i), :]
-        prod = (bf_nn(y_hl[rows_of(i), :], lo_hi) + bf_nn(left, mid_mid)) + bf_nn(left, hi_hi)
-        out_ref[rows_of(i), :] = a_ref[rows_of(i), :] - prod
+        tau_out[...] = tau_ref[...]
+        tf_out[...] = tf_ref[...]
+        for first in range(0, local_cols, ROWS):
+            hi, mid, lo = split3(yt_ref[first:first + ROWS, :])
+            y_parts[first:first + ROWS, :] = jnp.concatenate([hi, lo, mid, mid, hi, hi], axis=1)
+
+    for lane in range(0, tile, ROWS):
+        hi, mid, lo = split3(vt_ref[:, lane:lane + ROWS])
+        vt_parts = jnp.concatenate([lo, hi, mid, hi, mid, hi], axis=0)
+        for first in range(0, local_cols, ROWS):
+            prod = bf_nn(y_parts[first:first + ROWS, :], vt_parts)
+            out_ref[first:first + ROWS, lane:lane + ROWS] = a_ref[first:first + ROWS, lane:lane + ROWS] - prod
     out_ref[0:block_width, :] = vt_ref[own, :]
 
     @pl.when((lax.axis_index('row') == 0) & (pl.program_id(0) == 0))
@@ -571,20 +608,24 @@
         out_ref[0:block_width, 0:n] = rvt_ref[own, :]
 
 
-def update(a_t, vt, yt, rvt, block_width, tile=512):
+def update(a_t, vt, yt, rvt, tau_line, tfac, block_width, tile=1024):
     local_cols, local_rows = a_t.shape
     n = vt.shape[0]
+    once = lambda i: (0, 0)
     return pl.pallas_call(
         functools.partial(update_kernel, block_width),
-        out_shape=jax.ShapeDtypeStruct(a_t.shape, jnp.float32),
+        out_shape=(jax.ShapeDtypeStruct(a_t.shape, jnp.float32), jax.ShapeDtypeStruct(tau_line.shape, jnp.float32),
+                   jax.ShapeDtypeStruct(tfac.shape, jnp.float32)),
         grid=(local_rows // tile,),
         in_specs=[pl.BlockSpec((local_cols, tile), lambda i: (0, i)), pl.BlockSpec((n, tile), lambda i: (0, i)),
-                  pl.BlockSpec((local_cols, n), lambda i: (0, 0)), pl.BlockSpec((n, n), lambda i: (0, 0))],
-        out_specs=pl.BlockSpec((local_cols, tile), lambda i: (0, i)),
-        scratch_shapes=[pltpu.VMEM((local_cols, 2 * n), jnp.bfloat16)] * 2,
+                  pl.BlockSpec((local_cols, n), once), pl.BlockSpec((n, n), once), pl.BlockSpec((1, n), once),
+                  pl.BlockSpec(tfac.shape, lambda i: (0, 0, 0))],
+        out_specs=[pl.BlockSpec((local_cols, tile), lambda i: (0, i)), pl.BlockSpec((1, n), once),
+                   pl.BlockSpec(tfac.shape, lambda i: (0, 0, 0))],
+        scratch_shapes=[pltpu.VMEM((local_cols, 6 * n), jnp.bfloat16)],
         compiler_params=pltpu.CompilerParams(dimension_semantics=('arbitrary',), vmem_limit_bytes=56 * 1024 * 1024),
         name='update',
-    )(a_t, vt, yt, rvt)
+    )(a_t, vt, yt, rvt, tau_line, tfac)
 
 
 def solution(mesh):
@@ -598,18 +639,15 @@
         width = PANELS * block_width
         local_cols = local_blocks * block_width
         a_t = a_local.transpose(1, 2, 0).reshape(local_cols, local_rows)
-        kept, vt, yt, rvt, tau_line, t_full, flag = front(a_t, row_count, block_width)
-        out_t = update(a_t, vt, yt, rvt, block_width)
-        tfac = jnp.stack([t_full[s:s + block_width, s:s + block_width] for s in range(0, width, block_width)])
-
+        kept, vt, yt, rvt, tau_line, tfac, redo = front(a_t, row_count, block_width)
+        out_t, tau_line, tfac = update(a_t, vt, yt, rvt, tau_line, tfac, block_width)
         def column_form(state):
             kept = state[4]
             a_local = kept.reshape(local_blocks, block_width, local_rows).transpose(2, 0, 1)
             a_out, tau, tfac = columnwise_qr(a_local, col_count, row_count)
             return jnp.int32(0), a_out.transpose(1, 2, 0).reshape(local_cols, local_rows), tau, tfac, kept
 
-        redo = jnp.where(flag[0, 0] > 0.5, 0, 1).astype(jnp.int32)
-        state = (redo, out_t, tau_line[0], tfac, kept)
+        state = (redo[0, 0], out_t, tau_line[0], tfac, kept)
         _, out_t, tau, tfac, _ = lax.while_loop(lambda state: state[0] > 0, column_form, state)
         return out_t.reshape(local_blocks, block_width, local_rows).transpose(2, 0, 1), tau, tfac
 

time: 101 us -> 78.1 us (0.77)
  Pallas kernels: 95.5 us -> 76.4 us
  local copies, waits for them, and re-layouts: 3.21 us -> 0 us
    pallas_call x1, Pallas kernels: 76.8 us -> 60.9 us  [front(): pl.pallas_call(functools.partial(front_kernel, row_count, block_width), o...]
    pallas_call x1, Pallas kernels: 18.7 us -> 15.5 us  [update(): pl.pallas_call(functools.partial(update_kernel, block_width), out_shape=(...]
    slice x1 -> x0, local copies, waits for them, and re-layouts: 1.19 us -> none  [device_fn(): redo = jnp.where(flag[0, 0] > 0.5, 0, 1).astype(jnp.int32)]
    unnamed x1 -> x0, local copies, waits for them, and re-layouts: 1.17 us -> none
where the time goes in v2:
time: 78.1 us; the launch traced here: 78 us
  Pallas kernels  76.4 us (98%)
  between operations  0.8 us (1%)
    pallas_call x1, Pallas kernels, front(): pl.pallas_call(functools.partial(front_kernel, row_count, block_width), o...  60.9 us
    pallas_call x1, Pallas kernels, update(): pl.pallas_call(functools.partial(update_kernel, block_width), out_shape=(...  15.5 us

profile of v2, /device:TPU:97, one launch (start us, length us, event | category | flops | bytes accessed | tf_op | source)
XLA Modules:
  0.0 78.0 jit_solution(5647728951937096139)
XLA Ops:
  0.6 60.9 %front.1 = (f32[1024,4096]{1,0:T(8,128)}, f32[128,4096]{1,0:T(8,128)}, f32[1024,128]{1,0:T(8,128)}, f32[128,128]{1,0:T(8,128)}, f32[1,128]{1,0:T(1,128)}, /*index=5*/f32[4,32,32]{2,1,0:T(8,128)}, s32[1,1]{1,0:T(1,128)}) custom-call(f32[1024,4096]{1,0:T(8,128)} %bitcast.145), custom_call_target="tpu_custom_call" | custom-call | tf_op jit(solution)/shard_map/front/pallas_call | solution.py:562
  61.6 15.5 %update.1 = (f32[1024,4096]{1,0:T(8,128)}, f32[1,128]{1,0:T(1,128)}, f32[4,32,32]{2,1,0:T(8,128)}) custom-call(f32[1024,4096]{1,0:T(8,128)} %bitcast.146, f32[128,4096]{1,0:T(8,128)} %get-tuple-element.490.vt_ref, f32[1024,128]{1,0:T(8,128)} %get-tuple-element.491.yt_ref, f32[128,128]{1,0:T(8,128)} %get-tuple-element.492.rvt_ref, ...), custom_call_target="tpu_custom_call" | custom-call | tf_op jit(solution)/shard_map/update/pallas_call | solution.py:615
  77.1 0.7 while.76

commit v3 on v2

--- a/solution.py
+++ b/solution.py
@@ -251,10 +251,10 @@
     return lax.fori_loop(0, n // 8, step, jnp.zeros((1, n), jnp.float32))
 
 
-def front_kernel(row_count, block_width, a_hbm, a_copy, vt_out, yt_out, rvt_out, tau_out, tf_out, flag_out,
-                 a_buf, lead, ct_acc, g_acc, g_send, g_recv, g_part, g_all, c_recv, top_t, a11_t, yt_buf, max_buf,
+def front_kernel(row_count, block_width, a_hbm, a_copy, a_buf, vt_hbm, yt_out, rvt_out, tau_out, tf_out, flag_out,
+                 lead, ct_acc, g_acc, g_send, g_recv, g_part, g_all, c_recv, top_t, a11_t, yt_buf, max_buf,
                  w1_ref, w2_ref, vinv_ref, v_ref, r_ref, u_ref,
-                 own_sem, load_sem, keep_sem, right_send, left_send, fwd_send, from_left, from_right, fwd_recv,
+                 vt_out, vt_sem, own_sem, load_sem, keep_sem, right_send, left_send, fwd_send, from_left, from_right, fwd_recv,
                  max_send, max_recv, a11_send, a11_recv, top_send, top_recv,
                  gs_send, gs_recv, ga_send, ga_recv, cs_send, cs_recv, y_send, y_recv):
     local_cols, local_rows = a_hbm.shape
@@ -518,6 +518,8 @@
     def _():
         vt_out[:, 0:n] = jnp.where(lane_ids > row_ids, rv_t, eye)
 
+    vt_copy = pltpu.make_async_copy(vt_out, vt_hbm, vt_sem)
+    vt_copy.start()
     for step in range(2, row_count, 2):
         y_arrive(lax.rem(row_rank + row_count - step, row_count), step)
         y_pass(step).start()
@@ -525,6 +527,7 @@
     for step in range(2, row_count, 2):
         y_arrive(lax.rem(partner + row_count - step, row_count), step + 1)
     yt_out[...] = yt_buf[...]
+    vt_copy.wait()
 
     @pl.loop(0, CHUNKS)
     def _(c):
@@ -561,23 +564,24 @@
     spec = pl.BlockSpec(memory_space=pltpu.VMEM)
     return pl.pallas_call(
         functools.partial(front_kernel, row_count, block_width),
-        out_shape=(jax.ShapeDtypeStruct(a_t.shape, f32), jax.ShapeDtypeStruct((n, local_rows), f32), jax.ShapeDtypeStruct((local_cols, n), f32), mat,
+        out_shape=(jax.ShapeDtypeStruct(a_t.shape, f32), jax.ShapeDtypeStruct(a_t.shape, f32), jax.ShapeDtypeStruct((n, local_rows), f32), jax.ShapeDtypeStruct((local_cols, n), f32), mat,
                    jax.ShapeDtypeStruct((1, n), f32), jax.ShapeDtypeStruct((PANELS, block_width, block_width), f32),
                    jax.ShapeDtypeStruct((1, 1), jnp.int32)),
         in_specs=[pl.BlockSpec(memory_space=pl.ANY)],
-        out_specs=[pl.BlockSpec(memory_space=pl.ANY)] + [spec] * 5 + [pl.BlockSpec(memory_space=pltpu.SMEM)],
+        out_specs=[pl.BlockSpec(memory_space=pl.ANY), spec, pl.BlockSpec(memory_space=pl.ANY)] + [spec] * 4 + [pl.BlockSpec(memory_space=pltpu.SMEM)],
         scratch_shapes=[
-            vmem((local_cols, local_rows), f32), vmem((n, local_rows), f32), vmem((local_cols, n), f32), vmem((n, n), f32),
+            vmem((n, local_rows), f32), vmem((local_cols, n), f32), vmem((n, n), f32),
             vmem((row_count, g_rows + 8, n), f32), vmem((row_count, g_rows + 8, n), f32), vmem((g_rows + 8, n), f32),
             vmem((row_count, g_rows + 8, n), f32), vmem((row_count, share, n), f32), vmem((share, n), f32), vmem((n, n), f32),
             vmem((local_cols, n), f32), vmem((4, 8, 128), f32),
             vmem((n, n), f32), vmem((n, n), f32), vmem((n, n), f32), vmem((n, n), f32), vmem((n, n), f32), vmem((n, n), f32),
+            vmem((n, local_rows), f32), sem,
             sem((CHUNKS,)), sem((CHUNKS,)), sem((CHUNKS,)), sem((CHUNKS,)), sem((CHUNKS,)), sem((CHUNKS,)), sem((CHUNKS,)), sem((CHUNKS,)), sem((CHUNKS,)),
             sem((4,)), sem((4,)), sem((row_count,)), sem, sem((row_count,)), sem,
             sem((row_count,)), sem((row_count,)), sem((row_count,)), sem((row_count,)),
             sem((row_count,)), sem((row_count,)), sem((row_count,)), sem((row_count,)),
         ],
-        compiler_params=pltpu.CompilerParams(collective_id=0, has_side_effects=True, vmem_limit_bytes=60 * 1024 * 1024),
+        compiler_params=pltpu.CompilerParams(collective_id=0, has_side_effects=True, vmem_limit_bytes=26 * 1024 * 1024),
         name='front',
     )(a_t)
 
@@ -596,11 +600,12 @@
             y_parts[first:first + ROWS, :] = jnp.concatenate([hi, lo, mid, mid, hi, hi], axis=1)
 
     for lane in range(0, tile, ROWS):
+        a_lanes = pl.ds(pl.multiple_of(pl.program_id(0) * tile + lane, ROWS), ROWS)
         hi, mid, lo = split3(vt_ref[:, lane:lane + ROWS])
         vt_parts = jnp.concatenate([lo, hi, mid, hi, mid, hi], axis=0)
         for first in range(0, local_cols, ROWS):
             prod = bf_nn(y_parts[first:first + ROWS, :], vt_parts)
-            out_ref[first:first + ROWS, lane:lane + ROWS] = a_ref[first:first + ROWS, lane:lane + ROWS] - prod
+            out_ref[first:first + ROWS, lane:lane + ROWS] = a_ref[first:first + ROWS, a_lanes] - prod
     out_ref[0:block_width, :] = vt_ref[own, :]
 
     @pl.when((lax.axis_index('row') == 0) & (pl.program_id(0) == 0))
@@ -617,13 +622,13 @@
         out_shape=(jax.ShapeDtypeStruct(a_t.shape, jnp.float32), jax.ShapeDtypeStruct(tau_line.shape, jnp.float32),
                    jax.ShapeDtypeStruct(tfac.shape, jnp.float32)),
         grid=(local_rows // tile,),
-        in_specs=[pl.BlockSpec((local_cols, tile), lambda i: (0, i)), pl.BlockSpec((n, tile), lambda i: (0, i)),
+        in_specs=[pl.BlockSpec(memory_space=pltpu.VMEM), pl.BlockSpec((n, tile), lambda i: (0, i)),
                   pl.BlockSpec((local_cols, n), once), pl.BlockSpec((n, n), once), pl.BlockSpec((1, n), once),
                   pl.BlockSpec(tfac.shape, lambda i: (0, 0, 0))],
         out_specs=[pl.BlockSpec((local_cols, tile), lambda i: (0, i)), pl.BlockSpec((1, n), once),
                    pl.BlockSpec(tfac.shape, lambda i: (0, 0, 0))],
         scratch_shapes=[pltpu.VMEM((local_cols, 6 * n), jnp.bfloat16)],
-        compiler_params=pltpu.CompilerParams(dimension_semantics=('arbitrary',), vmem_limit_bytes=56 * 1024 * 1024),
+        compiler_params=pltpu.CompilerParams(dimension_semantics=('arbitrary',), vmem_limit_bytes=26 * 1024 * 1024),
         name='update',
     )(a_t, vt, yt, rvt, tau_line, tfac)
 
@@ -639,8 +644,8 @@
         width = PANELS * block_width
         local_cols = local_blocks * block_width
         a_t = a_local.transpose(1, 2, 0).reshape(local_cols, local_rows)
-        kept, vt, yt, rvt, tau_line, tfac, redo = front(a_t, row_count, block_width)
-        out_t, tau_line, tfac = update(a_t, vt, yt, rvt, tau_line, tfac, block_width)
+        kept, a_near, vt, yt, rvt, tau_line, tfac, redo = front(a_t, row_count, block_width)
+        out_t, tau_line, tfac = update(a_near, vt, yt, rvt, tau_line, tfac, block_width)
         def column_form(state):
             kept = state[4]
             a_local = kept.reshape(local_blocks, block_width, local_rows).transpose(2, 0, 1)

time: 78.1 us -> 71.5 us (0.915)
  Pallas kernels: 76.4 us -> 69.8 us
    pallas_call x1, Pallas kernels: 15.5 us -> 9.88 us  [update(): pl.pallas_call(functools.partial(update_kernel, block_width), out_shape=(...]
    pallas_call x1, Pallas kernels: 60.9 us -> 59.9 us  [front(): pl.pallas_call(functools.partial(front_kernel, row_count, block_width), o...]
where the time goes in v3:
time: 71.5 us; the launch traced here: 71.4 us
  Pallas kernels  69.8 us (98%)
  loops' own time  0.81 us (1%)
  between operations  0.8 us (1%)
    pallas_call x1, Pallas kernels, front(): pl.pallas_call(functools.partial(front_kernel, row_count, block_width), o...  59.9 us
    pallas_call x1, Pallas kernels, update(): pl.pallas_call(functools.partial(update_kernel, block_width), out_shape=(...  9.88 us

profile of v3, /device:TPU:97, one launch (start us, length us, event | category | flops | bytes accessed | tf_op | source)
XLA Modules:
  0.0 71.4 jit_solution(10088567763847916887)
XLA Ops:
  0.6 59.9 %front.1 = (f32[1024,4096]{1,0:T(8,128)}, f32[1024,4096]{1,0:T(8,128)S(1)}, f32[128,4096]{1,0:T(8,128)S(1)}, f32[1024,128]{1,0:T(8,128)S(1)}, f32[128,128]{1,0:T...) custom-call(f32[1024,4096]{1,0:T(8,128)} %bitcast.145), custom_call_target="tpu_custom_call" | custom-call | tf_op jit(solution)/shard_map/front/pallas_call | solution.py:565
  60.5 9.9 %update.1 = (f32[1024,4096]{1,0:T(8,128)}, f32[1,128]{1,0:T(1,128)}, f32[4,32,32]{2,1,0:T(8,128)}) custom-call(f32[1024,4096]{1,0:T(8,128)S(1)} %get-tuple-element.491.a_ref, f32[128,4096]{1,0:T(8,128)S(1)} %get-tuple-element.492.vt_ref, f32[1024,128]{1,0:T(8,128)S(1)} %get-tuple-element.493.yt_ref, f32[128,128]{1,0:T(8,128)S(1)} %get-tuple-element.494.rvt_ref, ...), custom_call_target="tpu_custom_call" | custom-call | tf_op jit(solution)/shard_map/update/pallas_call | solution.py:620
  70.4 0.8 %while.76 = (s32[]{:T(128)}, f32[1024,4096]{1,0:T(8,128)}, f32[128]{0:T(128)}, f32[4,32,32]{2,1,0:T(8,128)}, f32[1024,4096]{1,0:T(8,128)}) while((s32[]{:T(128)}, f32[1024,4096]{1,0:T(8,128)}, f32[128]{0:T(128)}, f32[4,32,32]{2,1,0:T(8,128)}, f32[1024,4096]{1,0:T(8,128)}) %tuple.134), condition=%region_5.6_spmd, body=%region_0.5_spmd | while | flops 3298550272 | bytes 130490800 | solution.py:656
